TPU v7x, 32 devices: a whole 2x2x4 slice. The times are simulated.
32 devices in a mesh: groups: 2 (over x), owner: 16 (over z, y, core).
Axes of the slice: x: 2, y: 2, z: 4, core: 2. Of those that a mesh axis runs over, the one named last changes fastest.
Arguments:
- queries: bfloat16 [2048, 1024], P(('groups', 'owner')), parts along dimension 0, may hold values from -0.3984375 to 0.3984375
- probes: int32 [2048, 8], P(('groups', 'owner')), parts along dimension 0, may hold values from 0 to 255, as said below
- passages: bfloat16 [256, 256, 1024], P('owner'), may hold values from -6 to 6
- centroids: bfloat16 [256, 1024], P('owner'), may hold values from -6 to 6
- counts: int32 [256], P('owner'), may hold values from 1 to 256
Outputs:
- scores: float32 [2048, 8, 256], P(('groups', 'owner')), parts along dimension 0
- visits: int32 [2048], P(('groups', 'owner')), parts along dimension 0
There are 2 independent parts, one for each index of `groups`. A program takes and returns all parts, laid end to end along the dimension named above; an argument that names none is the same for every part. Nothing has to cross between parts.
Inputs may be any that keep to these rules, and one draw needn't show every extreme that they name: Cluster c belongs to owner index c // 16. In each aligned block of 64 queries (the queries of one index of owner) at most 64 probes name clusters of one owner, and in every draw some owners receive exactly 64 probes from every block. A query may name a cluster more than once.
All inputs are finite; a program needn't handle non-finite values.
Results may differ from a plain program's by a relative error of at most 0.0003.
Values may be sent and summed in bfloat16 or wider, within the bound.
A program may use at most 64 MiB of HBM per device.

v0:
```python
import jax
import jax.numpy as jnp
from jax import lax
from jax.sharding import PartitionSpec as P


def body(queries, probes, passages, centroids, counts):
    owner_count = lax.axis_size("owner")
    per_device, probe_count = probes.shape
    local_count, block_span, feature_width = passages.shape
    capacity = 2 * per_device * probe_count // owner_count
    pair_count = per_device * probe_count
    passage_blocks = jnp.transpose(passages, (0, 2, 1))
    flat_probes = probes.reshape(-1)
    target_owner = flat_probes // local_count
    target_local = flat_probes % local_count
    owner_hits = (
        target_owner[:, None] == jnp.arange(owner_count, dtype=jnp.int32)[None, :]
    ).astype(jnp.int32)
    slot_rank = jnp.sum((jnp.cumsum(owner_hits, axis=0) - owner_hits) * owner_hits, axis=1)
    slot_index = target_owner * capacity + slot_rank
    pair_ids = jnp.arange(pair_count, dtype=jnp.int32)
    slot_match = slot_index[None, :] == jnp.arange(owner_count * capacity, dtype=jnp.int32)[:, None]
    slot_filled = jnp.any(slot_match, axis=1)
    source_pair = jnp.sum(jnp.where(slot_match, pair_ids[None, :], 0), axis=1)
    send_rows = jnp.where(
        slot_filled[:, None], queries[source_pair // probe_count], jnp.zeros((), jnp.bfloat16)
    )
    send_ids = jnp.where(slot_filled, target_local[source_pair], -1)
    query_rows = lax.all_to_all(
        send_rows.reshape(owner_count, capacity, feature_width),
        "owner",
        split_axis=0,
        concat_axis=0,
        tiled=True,
    )
    cluster_ids = lax.all_to_all(
        send_ids.reshape(owner_count, capacity), "owner", split_axis=0, concat_axis=0, tiled=True
    )
    source_count, slot_count = cluster_ids.shape
    row_total = source_count * slot_count
    flat_rows = query_rows.reshape(row_total, feature_width)
    flat_ids = cluster_ids.reshape(-1)
    group_ids = jnp.where(flat_ids < 0, 0, flat_ids).astype(jnp.int32)
    cluster_pick = flat_ids[:, None] == jnp.arange(local_count, dtype=jnp.int32)[None, :]
    live_sizes = jnp.sum(jnp.where(cluster_pick, counts[None, :], 0), axis=1)
    group_pick = group_ids[:, None] == jnp.arange(local_count, dtype=jnp.int32)[None, :]
    group_sizes = jnp.sum(group_pick.astype(jnp.int32), axis=0)
    order = jnp.argsort(group_ids, stable=True)
    undo_order = jnp.argsort(order, stable=True)
    sorted_rows = flat_rows[order]
    sorted_scores = lax.ragged_dot(
        sorted_rows, passage_blocks, group_sizes, preferred_element_type=jnp.float32
    )
    own_scores = sorted_scores[undo_order]
    centre_term = jnp.einsum(
        "rd,rd->r", flat_rows, centroids[group_ids], preferred_element_type=jnp.float32
    )
    live_mask = jnp.arange(block_span, dtype=jnp.int32)[None, :] < live_sizes[:, None]
    masked_scores = jnp.where(live_mask, own_scores + centre_term[:, None], 0.0)
    back_scores = lax.all_to_all(
        masked_scores.reshape(source_count, slot_count, block_span),
        "owner",
        split_axis=0,
        concat_axis=0,
        tiled=True,
    )
    back_sizes = lax.all_to_all(
        live_sizes.astype(jnp.float32).reshape(source_count, slot_count),
        "owner",
        split_axis=0,
        concat_axis=0,
        tiled=True,
    )
    flat_scores = back_scores.reshape(owner_count * capacity, block_span)
    scores = flat_scores[slot_index].reshape(per_device, probe_count, block_span)
    pair_sizes = back_sizes.reshape(-1)[slot_index].reshape(per_device, probe_count)
    visits = jnp.sum(pair_sizes, axis=1).astype(jnp.int32)
    return (scores, visits)


def solution(mesh):
    in_specs = (
        P(("groups", "owner"), None),
        P(("groups", "owner"), None),
        P("owner", None, None),
        P("owner", None),
        P("owner"),
    )
    out_specs = (P(("groups", "owner"), None, None), P(("groups", "owner")))
    return jax.shard_map(body, mesh=mesh, in_specs=in_specs, out_specs=out_specs, check_vma=False)
```

profile of v0, /device:TPU:0, one launch (start us, length us, event | category | flops | bytes accessed | tf_op | source)
XLA Modules:
  0.0 144.8 jit_solution(9022562949180411143)
XLA Ops:
  0.6 0.8 copy.18
  1.7 1.2 reduce-window.6
  3.8 6.9 %gather_fusion = s32[1024]{0:T(1024)S(1)} fusion(s32[512]{0:T(512)S(1)} %get-tuple-element.12, s32[1024]{0:T(1024)S(1)} %broadcast_clamp_fusion.2), kind=kCustom, calls=%fused_computation | custom fusion | bytes 12288 | tf_op jit(solution)/shard_map/gather | solution.py:29
  10.7 0.7 select_n.145
  11.4 7.4 %all-to-all-start = ((s32[16,1,64]{2,1,0:T(1,128)}), s32[16,1,64]{2,1,0:T(1,128)S(1)}, u32[]{:S(2)}, u32[]{:S(2)}) async-start(s32[16,1,64]{2,1,0:T(1,128)} %select_n.145), calls=%async_computation | async-start | bytes 16384 | tf_op jit(solution)/shard_map/all_to_all | solution.py:37
  18.9 4.1 %gather_fusion.1 = bf16[1024,1024]{1,0:T(8,128)(2,1)S(1)} fusion(bf16[64,1024]{1,0:T(8,128)(2,1)S(1)} %copy-done, s32[1024]{0:T(1024)S(1)} %broadcast_clamp_fusion.1), kind=kCustom, calls=%fused_computation.1 | custom fusion | bytes 4198400 | tf_op jit(solution)/shard_map/gather | solution.py:27
  23.0 1.6 %broadcast_select_fusion = bf16[16,64,1024]{2,1,0:T(8,128)(2,1)} fusion(bf16[16,64,1024]{2,1,0:T(8,128)(2,1)S(1)} %bitcast.36, pred[16,64]{1,0:T(8,128)(4,1)S(1)} %broadcast_in_dim.77), kind=kLoop, calls=%fused_computation.12 | loop fusion | flops 1048576 | bytes 4195328 | tf_op jit(solution)/shard_map/jit(_where)/select_n | solution.py:26
  24.6 0.6 all-to-all-done
  25.2 5.4 %all-to-all-start.1 = ((bf16[16,64,1024]{2,1,0:T(8,128)(2,1)}), bf16[16,64,1024]{2,1,0:T(8,128)(2,1)S(1)}, u32[]{:S(2)}, u32[]{:S(2)}) async-start(bf16[16,64,1024]{2,1,0:T(8,128)(2,1)} %broadcast_select_fusion), calls=%async_computation.1 | async-start | bytes 4194304 | tf_op jit(solution)/shard_map/all_to_all | solution.py:30
  30.6 12.3 %copy.21 = bf16[16,256,1024]{1,2,0:T(8,128)(2,1)} copy(bf16[16,256,1024]{2,1,0:T(8,128)(2,1)} %param.7) | data formatting | bytes 16777216 | tf_op args[2]
  42.9 0.5 broadcast.357
  43.4 0.7 reduce.12
  44.4 4.4 %sort.31 = (s32[1024]{0:T(1024)}, s32[1024]{0:T(1024)S(1)}) sort(s32[1024]{0:T(1024)S(1)} %compare_select_fusion.6, s32[1024]{0:T(1024)S(1)} %iota.33), dimensions={0}, to_apply=%region_6.7 | sort | flops 10240 | bytes 16384 | tf_op jit(solution)/shard_map/jit(argsort)/sort | solution.py:49
  48.8 0.6 convert_reduce_fusion
  49.4 1.8 %ragged-dot-metadata = (s32[17]{0:T(128)}, s32[19]{0:T(128)}, s32[19]{0:T(128)}, s32[1]{0:T(128)}) custom-call(s32[16]{0:T(128)} %convert_reduce_fusion), custom_call_target="tpu_custom_call" | custom-call | tf_op ragged-dot-metadata
  51.2 0.7 convert_element_type.31
  51.9 4.4 %sort.32 = (s32[1024]{0:T(1024)}, s32[1024]{0:T(1024)S(1)}) sort(s32[1024]{0:T(1024)S(1)} %get-tuple-element.4, s32[1024]{0:T(1024)S(1)} %iota.34), dimensions={0}, to_apply=%region_8.9 | sort | flops 10240 | bytes 16384 | tf_op jit(solution)/shard_map/jit(argsort)/sort | solution.py:50
  56.3 5.4 %gather_fusion.4 = bf16[1024,1024]{1,0:T(8,128)(2,1)} fusion(bf16[16,1024]{1,0:T(8,128)(2,1)S(1)} %copy-done.1, s32[1024]{0:T(1024)S(1)} %broadcast_clamp_fusion), kind=kCustom, calls=%fused_computation.4 | custom fusion | bytes 4198400 | tf_op jit(solution)/shard_map/gather | solution.py:57
  61.7 9.9 %all-to-all-done.1 = bf16[16,64,1024]{2,1,0:T(8,128)(2,1)S(1)} async-done(((bf16[16,64,1024]{2,1,0:T(8,128)(2,1)}), bf16[16,64,1024]{2,1,0:T(8,128)(2,1)S(1)}, u32[]{:S(2)}, u32[]{:S(2)}) %all-to-all-start.1) | async-done | bytes 2097184 | tf_op jit(solution)/shard_map/all_to_all | solution.py:30
  71.6 11.2 %all-to-all-start.3 = ((f32[16,1,64]{2,1,0:T(1,128)}), f32[16,1,64]{2,1,0:T(1,128)S(1)}, u32[]{:S(2)}, u32[]{:S(2)}) async-start(f32[16,1,64]{2,1,0:T(1,128)} %convert_element_type.31), calls=%async_computation.3 | async-start | bytes 16384 | tf_op jit(solution)/shard_map/all_to_all | solution.py:68
  82.8 2.2 %fusion = f32[1024]{0:T(1024)S(1)} fusion(bf16[1024,1024]{1,0:T(8,128)(2,1)} %gather_fusion.4, bf16[16,64,1024]{2,1,0:T(8,128)(2,1)S(1)} %all-to-all-done.1), kind=kLoop, calls=%fused_computation.8 | loop fusion | flops 4193280 | bytes 4198400 | tf_op jit(solution)/shard_map/rd,rd->r/dot_general | solution.py:56
  85.1 5.4 %gather_fusion.2 = bf16[1024,1024]{1,0:T(8,128)(2,1)} fusion(bf16[1024,1024]{1,0:T(8,128)(2,1)S(1)} %bitcast.33, s32[1024]{0:T(1024)S(1)} %fusion.6), kind=kCustom, calls=%fused_computation.2 | custom fusion | bytes 4198400 | tf_op jit(solution)/shard_map/gather | solution.py:51
  90.5 17.0 %ragged-dot-none = f32[1024,256]{1,0:T(8,128)} custom-call(s32[1]{0:T(128)} %get-tuple-element.6, s32[17]{0:T(128)} %get-tuple-element.7, s32[19]{0:T(128)} %get-tuple-element.8, s32[19]{0:T(128)} %get-tuple-element.9, s32[1]{0:T(128)} %get-tuple-element.6, bf16[1024,1024]{1,0:T(8,128)(2,1)} %gather_fusion.2, bf16[16,1024,256]{2,1,0:T(8,128)(2,1)} %bitcast.34), custom_call_target="tpu_custom_call" | custom-call | flops 536870912 | bytes 11534400 | tf_op jit(solution)/shard_map/ragged_dot_general/ragged-dot-none
  107.5 4.7 %gather_fusion.3 = f32[1024,256]{1,0:T(8,128)S(1)} fusion(f32[1024,256]{1,0:T(8,128)} %ragged-dot-none, s32[1024]{0:T(1024)S(1)} %fusion.7), kind=kCustom, calls=%fused_computation.3 | custom fusion | bytes 2101248 | tf_op jit(solution)/shard_map/gather | solution.py:55
  112.2 1.3 add_select_fusion
  113.5 6.1 %all-to-all-start.2 = ((f32[16,64,256]{2,1,0:T(8,128)}), f32[16,64,256]{2,1,0:T(8,128)S(1)}, u32[]{:S(2)}, u32[]{:S(2)}) async-start(f32[16,64,256]{2,1,0:T(8,128)} %add_select_fusion), calls=%async_computation.2 | async-start | bytes 2097152 | tf_op jit(solution)/shard_map/all_to_all | solution.py:61
  119.8 0.5 broadcast.358
  120.3 0.7 reduce.13
  121.1 2.3 %gather_fusion.6 = f32[512]{0:T(512)S(1)} fusion(f32[1024]{0:T(1024)S(1)} %reshape.359, s32[1024]{0:T(1024)S(1)} %pad_clamp_fusion), kind=kCustom, calls=%fused_computation.6 | custom fusion | bytes 6144 | tf_op jit(solution)/shard_map/gather | solution.py:77
  123.5 0.5 convert_element_type.32
  124.1 18.5 %all-to-all-done.2 = f32[16,64,256]{2,1,0:T(8,128)S(1)} async-done(((f32[16,64,256]{2,1,0:T(8,128)}), f32[16,64,256]{2,1,0:T(8,128)S(1)}, u32[]{:S(2)}, u32[]{:S(2)}) %all-to-all-start.2) | async-done | bytes 1048608 | tf_op jit(solution)/shard_map/all_to_all | solution.py:61
  142.5 2.2 %gather_fusion.5 = f32[512,256]{1,0:T(8,128)} fusion(f32[1024,256]{1,0:T(8,128)S(1)} %bitcast.35, s32[1024]{0:T(1024)S(1)} %pad_clamp_fusion), kind=kCustom, calls=%fused_computation.5 | custom fusion | bytes 1050624 | tf_op jit(solution)/shard_map/gather | solution.py:76
  (43 shorter events, 2.1 us)
Async XLA Ops:
  0.6 18.3 %copy-start = (bf16[64,1024]{1,0:T(8,128)(2,1)S(1)}, bf16[64,1024]{1,0:T(8,128)(2,1)}, u32[]{:S(2)}) copy-start(bf16[64,1024]{1,0:T(8,128)(2,1)} %param.5) | copy-start | bytes 393220
  11.4 13.8 %all-to-all-start = ((s32[16,1,64]{2,1,0:T(1,128)}), s32[16,1,64]{2,1,0:T(1,128)S(1)}, u32[]{:S(2)}, u32[]{:S(2)}) async-start(s32[16,1,64]{2,1,0:T(1,128)} %select_n.145), calls=%async_computation | async-start | bytes 16384 | tf_op jit(solution)/shard_map/all_to_all | solution.py:37
  25.2 46.4 %all-to-all-start.1 = ((bf16[16,64,1024]{2,1,0:T(8,128)(2,1)}), bf16[16,64,1024]{2,1,0:T(8,128)(2,1)S(1)}, u32[]{:S(2)}, u32[]{:S(2)}) async-start(bf16[16,64,1024]{2,1,0:T(8,128)(2,1)} %broadcast_select_fusion), calls=%async_computation.1 | async-start | bytes 4194304 | tf_op jit(solution)/shard_map/all_to_all | solution.py:30
  30.6 13.6 %copy-start.2 = (s32[16]{0:T(128)S(1)}, s32[16]{0:T(128)}, u32[]{:S(2)}) copy-start(s32[16]{0:T(128)} %param.9) | copy-start | bytes 196
  42.9 13.4 %copy-start.1 = (bf16[16,1024]{1,0:T(8,128)(2,1)S(1)}, bf16[16,1024]{1,0:T(8,128)(2,1)}, u32[]{:S(2)}) copy-start(bf16[16,1024]{1,0:T(8,128)(2,1)} %param.8) | copy-start | bytes 98308
  71.6 41.9 %all-to-all-start.3 = ((f32[16,1,64]{2,1,0:T(1,128)}), f32[16,1,64]{2,1,0:T(1,128)S(1)}, u32[]{:S(2)}, u32[]{:S(2)}) async-start(f32[16,1,64]{2,1,0:T(1,128)} %convert_element_type.31), calls=%async_computation.3 | async-start | bytes 16384 | tf_op jit(solution)/shard_map/all_to_all | solution.py:68
  113.5 29.0 %all-to-all-start.2 = ((f32[16,64,256]{2,1,0:T(8,128)}), f32[16,64,256]{2,1,0:T(8,128)S(1)}, u32[]{:S(2)}, u32[]{:S(2)}) async-start(f32[16,64,256]{2,1,0:T(8,128)} %add_select_fusion), calls=%async_computation.2 | async-start | bytes 2097152 | tf_op jit(solution)/shard_map/all_to_all | solution.py:61
where the time goes:
time: 147 us; the launch traced here: 145 us
  local copies, waits for them, and re-layouts  47.4 us (32%)
  starting transfers between devices  30.2 us (21%)
  waiting for transfers between devices  29 us (20%)
  Pallas kernels  18.8 us (13%)
  other arithmetic  18.6 us (13%)
    all_to_all x1, waiting for transfers between devices, body(): lax.all_to_all(masked_scores.reshape(source_count, slot_count, block_span...  18.5 us
    another operation x1, Pallas kernels  17 us
    unnamed x8, local copies, waits for them, and re-layouts  13.1 us
    all_to_all x1, starting transfers between devices, body(): lax.all_to_all(live_sizes.astype(jnp.float32).reshape(source_count, slot_...  11.2 us
    all_to_all x1, waiting for transfers between devices, body(): lax.all_to_all(send_rows.reshape(owner_count, capacity, feature_width), '...  9.9 us
    all_to_all x1, starting transfers between devices, body(): lax.all_to_all(send_ids.reshape(owner_count, capacity), 'owner', split_ax...  7.41 us
    gather x1, local copies, waits for them, and re-layouts, body(): send_ids = jnp.where(slot_filled, target_local[source_pair], -1)  6.87 us
    all_to_all x1, starting transfers between devices, body(): lax.all_to_all(masked_scores.reshape(source_count, slot_count, block_span...  6.14 us
  transfers between devices with their start and end apart: 4, of which 3 were waited for; matrix products, arithmetic and copies ran while one was open for 37% of the time, Pallas kernels for 13%

commit v1 on v0

--- a/solution.py
+++ b/solution.py
@@ -1,10 +1,12 @@
 import jax
 import jax.numpy as jnp
 from jax import lax
+from jax.experimental import pallas as pl
+from jax.experimental.pallas import tpu as pltpu
 from jax.sharding import PartitionSpec as P
 
 
-def body(queries, probes, passages, centroids, counts):
+def routed_body(queries, probes, passages, centroids, counts):
     owner_count = lax.axis_size("owner")
     per_device, probe_count = probes.shape
     local_count, block_span, feature_width = passages.shape
@@ -79,6 +81,360 @@
     return (scores, visits)
 
 
+LANES = 128
+TOP = 32767.0
+
+
+def owner_kernel(
+    n, q_ref, meta_ref, slot_ref, probe_ref, pass_ref, cent_ref, cnt_ref,
+    out_ref, vis_ref,
+    pass_v, qs, ms, dense, picked, sendb, sends, recvb, recvs, code_s, cnt_s, scale_s,
+    pass_sem, qsend, msend, qrecv, mrecv, bsend, ssend, brecv, srecv, loc_sem,
+):
+    clusters, span, width = pass_ref.shape
+    per_device, probe_count, _ = out_ref.shape
+    planes = n // 4
+    rows = 4 * per_device
+    meta_rows, _, lane_count = meta_ref.shape
+    cap = lane_count // 4
+    half = span // 2
+    me = lax.axis_index("owner")
+    z = me // 4
+    y = (me // 2) % 2
+    c = me % 2
+    y_dev = z * 4 + (1 - y) * 2 + c
+    c_dev = z * 4 + y * 2 + (1 - c)
+    has_low = z > 0
+    has_high = z < planes - 1
+
+    for k in range(clusters):
+        pltpu.make_async_copy(pass_ref.at[k], pass_v.at[k], pass_sem.at[k]).start()
+
+    barrier = pltpu.get_barrier_semaphore()
+
+    def greet(dev):
+        pl.semaphore_signal(barrier, inc=1, device_id={"owner": dev})
+
+    greet(y_dev)
+    greet(c_dev)
+
+    @pl.when(has_low)
+    def _():
+        greet(me - 4)
+
+    @pl.when(has_high)
+    def _():
+        greet(me + 4)
+
+    pl.semaphore_wait(barrier, 2 + jnp.where(has_low, 1, 0) + jnp.where(has_high, 1, 0))
+
+    def pair(s, target, dev, own=False):
+        return (
+            pltpu.make_async_remote_copy(
+                src_ref=meta_ref if own else ms.at[s], dst_ref=ms.at[s],
+                send_sem=msend.at[s, target], recv_sem=mrecv.at[s], device_id={"owner": dev},
+            ),
+            pltpu.make_async_remote_copy(
+                src_ref=q_ref if own else qs.at[s], dst_ref=qs.at[s],
+                send_sem=qsend.at[s, target], recv_sem=qrecv.at[s], device_id={"owner": dev},
+            ),
+        )
+
+    def push(s, target, dev, own=False):
+        for copy in pair(s, target, dev, own):
+            copy.start()
+
+    def drain(s, target, dev, own=False):
+        for copy in pair(s, target, dev, own):
+            copy.wait_send()
+
+    def arrive(s):
+        for copy in pair(s, 0, c_dev):
+            copy.wait_recv()
+
+    def onward(act, s, low, high, own=False):
+        @pl.when(low)
+        def _():
+            act(s, 0, me - 4, own)
+
+        @pl.when(high)
+        def _():
+            act(s, 1, me + 4, own)
+
+        act(s, 2, y_dev, own)
+        act(s, 3, c_dev, own)
+
+    onward(push, me, has_low, has_high, True)
+    qs[me] = q_ref[...]
+    ms[me] = meta_ref[...]
+
+    near = jnp.minimum(z, planes - 1 - z)
+    long_side = jnp.where(z < planes - 1 - z, 1, -1)
+
+    def plane_of(k):
+        both = jnp.where(k % 2 == 1, -1, 1) * ((k + 1) // 2)
+        return z + jnp.where(k <= 2 * near, both, long_side * (k - near))
+
+    def relay_z(k, act=push, wait=True):
+        p = plane_of(k)
+        s = p * 4 + y * 2 + c
+        if wait:
+            arrive(s)
+        onward(act, s, (p > z) & has_low, (p < z) & has_high)
+
+    def relay_y(k):
+        s = plane_of(k) * 4 + (1 - y) * 2 + c
+        arrive(s)
+        push(s, 3, c_dev)
+
+    def back_pair(s):
+        return (
+            pltpu.make_async_remote_copy(
+                src_ref=sendb.at[s], dst_ref=recvb.at[me],
+                send_sem=bsend.at[s], recv_sem=brecv.at[me], device_id={"owner": s},
+            ),
+            pltpu.make_async_remote_copy(
+                src_ref=sends.at[s // 4], dst_ref=recvs.at[me],
+                send_sem=ssend.at[s], recv_sem=srecv.at[me], device_id={"owner": s},
+            ),
+        )
+
+    def to_scalar(s):
+        return (
+            pltpu.make_async_copy(ms.at[s, me // 4], code_s.at[s], loc_sem.at[0, s]),
+            pltpu.make_async_copy(ms.at[s, meta_rows - 1], cnt_s.at[s], loc_sem.at[1, s]),
+        )
+
+    def compute(k):
+        p = plane_of(k)
+        base = p * 4
+        for i in range(4):
+            for copy in to_scalar(base + i):
+                copy.start()
+        block = qs[pl.ds(base, 4)].reshape(rows, width)
+        centre = lax.dot_general(
+            block, cent_ref[...], (((1,), (1,)), ((), ())), preferred_element_type=jnp.float32
+        )
+        lane = lax.broadcasted_iota(jnp.int32, centre.shape, 1)
+        slot_lane = lax.broadcasted_iota(jnp.int32, (1, span), 1)
+
+        def one_cluster(cl, carry):
+            @pl.when(k == 0)
+            def _():
+                pltpu.make_async_copy(pass_ref.at[cl], pass_v.at[cl], pass_sem.at[cl]).wait()
+
+            direct = lax.dot_general(
+                qs[pl.ds(base, 4)].reshape(rows, width), pass_v[cl],
+                (((1,), (1,)), ((), ())), preferred_element_type=jnp.float32,
+            )
+            term = jnp.sum(jnp.where(lane == cl, centre, 0.0), axis=1, keepdims=True)
+            dense[pl.ds(pl.multiple_of(cl * rows, rows), rows), :] = jnp.where(
+                slot_lane < cnt_ref[cl], direct + term, 0.0
+            )
+            return carry
+
+        lax.fori_loop(0, clusters, one_cluster, 0)
+        for i in range(4):
+            for copy in to_scalar(base + i):
+                copy.wait()
+        for i in range(4):
+            code_lane = (me % 4) * cap
+
+            def eight(g, carry):
+                for u in range(8):
+                    k_slot = g * 8 + u
+                    row = code_s[base + i, 0, code_lane + k_slot] + i * per_device
+                    picked[pl.ds(i * cap + k_slot, 1), :] = dense[pl.ds(row, 1), :]
+                return carry
+
+            lax.fori_loop(0, cap // 8, eight, 0)
+        found = picked[...]
+        top = jnp.maximum(jnp.max(jnp.abs(found), axis=1, keepdims=True), 1e-30)
+        coded = jnp.round(found * (TOP / top)).astype(jnp.int32)
+        packed = (coded[:, half:] << 16) | (coded[:, :half] & 0xFFFF)
+        sendb[pl.ds(base, 4)] = packed.reshape(4, cap, half)
+        wide = jnp.broadcast_to(top * (1.0 / TOP), (4 * cap, LANES))
+        sends[p] = jnp.transpose(wide)[0:1, :]
+        for i in range(4):
+            s = base + i
+
+            @pl.when(s == me)
+            def _():
+                recvb[me] = sendb[me]
+                recvs[me] = sends[p]
+
+            @pl.when(s != me)
+            def _():
+                for copy in back_pair(s):
+                    copy.start()
+
+    ahead = 1 + jnp.where(near >= 1, 1, 0)
+
+    def step(k, carry):
+        @pl.when((k == 0) & (planes > 1))
+        def _():
+            relay_z(1)
+
+        @pl.when((k == 0) & (ahead > 1))
+        def _():
+            relay_z(2)
+
+        @pl.when((k > 0) & (k + ahead < planes))
+        def _():
+            relay_z(k + ahead)
+
+        relay_y(k)
+        p = plane_of(k)
+        arrive(p * 4 + y * 2 + (1 - c))
+        arrive(p * 4 + (1 - y) * 2 + (1 - c))
+        compute(k)
+        return carry
+
+    lax.fori_loop(0, planes, step, 0)
+
+    def collect(s, carry):
+        @pl.when(s != me)
+        def _():
+            for copy in (
+                pltpu.make_async_remote_copy(
+                    src_ref=sendb.at[s], dst_ref=recvb.at[s],
+                    send_sem=bsend.at[s], recv_sem=brecv.at[s], device_id={"owner": c_dev},
+                ),
+                pltpu.make_async_remote_copy(
+                    src_ref=sends.at[s // 4], dst_ref=recvs.at[s],
+                    send_sem=ssend.at[s], recv_sem=srecv.at[s], device_id={"owner": c_dev},
+                ),
+            ):
+                copy.wait_recv()
+
+        return carry
+
+    lax.fori_loop(0, n, collect, 0)
+    scale_copy = pltpu.make_async_copy(recvs, scale_s, loc_sem.at[0, 0])
+    scale_copy.start()
+    scale_copy.wait()
+
+    def one_query(q, carry):
+        visited = jnp.int32(0)
+        for j in range(probe_count):
+            slot = slot_ref[q * probe_count + j]
+            probe = probe_ref[q * probe_count + j]
+            owner = slot // cap
+            kept = slot % cap
+            scale = scale_s[owner, 0, (me % 4) * cap + kept]
+            word = recvb[owner, pl.ds(kept, 1), :]
+            low = (word << 16) >> 16
+            out_ref[q, j : j + 1, :half] = low.astype(jnp.float32) * scale
+            out_ref[q, j : j + 1, half:] = (word >> 16).astype(jnp.float32) * scale
+            visited = visited + cnt_s[probe // clusters, 0, probe % clusters]
+        vis_ref[q] = visited
+        return carry
+
+    lax.fori_loop(0, per_device, one_query, 0)
+
+    onward(drain, me, has_low, has_high, True)
+
+    def finish(k, carry):
+        @pl.when(k > 0)
+        def _():
+            relay_z(k, drain, False)
+
+        drain(plane_of(k) * 4 + (1 - y) * 2 + c, 3, c_dev)
+        return carry
+
+    lax.fori_loop(0, planes, finish, 0)
+
+    def finish_back(s, carry):
+        @pl.when(s != me)
+        def _():
+            for copy in back_pair(s):
+                copy.wait_send()
+
+        return carry
+
+    lax.fori_loop(0, n, finish_back, 0)
+
+
+def slot_tables(flat_probes, n, cap, clusters, per_device, probe_count):
+    pair_count = flat_probes.shape[0]
+    owner = flat_probes // clusters
+    local = flat_probes % clusters
+    pair = jnp.arange(pair_count, dtype=jnp.int32)
+    same = (owner[:, None] == owner[None, :]) & (pair[None, :] < pair[:, None])
+    slot = owner * cap + jnp.sum(same.astype(jnp.int32), axis=1)
+    code = local * (4 * per_device) + pair // probe_count
+    hit = slot[None, :] == jnp.arange(n * cap, dtype=jnp.int32)[:, None]
+    table = jnp.sum(jnp.where(hit, code[None, :], 0), axis=1)
+    return slot, table
+
+
+def fused_body(queries, probes, passages, centroids, counts):
+    n = lax.axis_size("owner")
+    per_device, probe_count = probes.shape
+    clusters, span, width = passages.shape
+    cap = 2 * per_device * probe_count // n
+    flat = probes.reshape(-1)
+    slot, table = slot_tables(flat, n, cap, clusters, per_device, probe_count)
+    lane_count = 4 * cap
+    count_row = jnp.pad(counts, (0, lane_count - clusters)).reshape(1, 1, lane_count)
+    meta = jnp.concatenate([table.reshape(n // 4, 1, lane_count), count_row], axis=0)
+    vmem = pl.BlockSpec(memory_space=pltpu.VMEM)
+    smem = pl.BlockSpec(memory_space=pltpu.SMEM)
+    dma = pltpu.SemaphoreType.DMA
+    rows = 4 * per_device
+    half = span // 2
+    return pl.pallas_call(
+        lambda *refs: owner_kernel(n, *refs),
+        out_shape=(
+            jax.ShapeDtypeStruct((per_device, probe_count, span), jnp.float32),
+            jax.ShapeDtypeStruct((per_device,), jnp.int32),
+        ),
+        in_specs=[vmem, vmem, smem, smem, pl.BlockSpec(memory_space=pl.ANY), vmem, smem],
+        out_specs=(vmem, smem),
+        scratch_shapes=[
+            pltpu.VMEM((clusters, span, width), jnp.bfloat16),
+            pltpu.VMEM((n, per_device, width), jnp.bfloat16),
+            pltpu.VMEM((n, n // 4 + 1, 1, lane_count), jnp.int32),
+            pltpu.VMEM((clusters * rows, span), jnp.float32),
+            pltpu.VMEM((4 * cap, span), jnp.float32),
+            pltpu.VMEM((n, cap, half), jnp.int32),
+            pltpu.VMEM((n // 4, 1, lane_count), jnp.float32),
+            pltpu.VMEM((n, cap, half), jnp.int32),
+            pltpu.VMEM((n, 1, lane_count), jnp.float32),
+            pltpu.SMEM((n, 1, lane_count), jnp.int32),
+            pltpu.SMEM((n, 1, lane_count), jnp.int32),
+            pltpu.SMEM((n, 1, lane_count), jnp.float32),
+            dma((clusters,)),
+            dma((n, 4)),
+            dma((n, 4)),
+            dma((n,)),
+            dma((n,)),
+            dma((n,)),
+            dma((n,)),
+            dma((n,)),
+            dma((n,)),
+            dma((2, n)),
+        ],
+        compiler_params=pltpu.CompilerParams(
+            collective_id=0, has_side_effects=True, vmem_limit_bytes=48 * 2**20
+        ),
+    )(queries, meta, slot, flat, passages, centroids, counts)
+
+
+def body(queries, probes, passages, centroids, counts):
+    n = lax.axis_size("owner")
+    per_device, probe_count = probes.shape
+    clusters, span, width = passages.shape
+    lane_count = 8 * per_device * probe_count // n
+    held = clusters * span * (2 * width + 16 * per_device) + 2 * n * per_device * width
+    fits = (
+        n % 4 == 0 and n >= 8 and lane_count % LANES == 0 and lane_count >= clusters
+        and span % (2 * LANES) == 0 and held < 32 * 2**20
+    )
+    chosen = fused_body if fits else routed_body
+    return chosen(queries, probes, passages, centroids, counts)
+
+
 def solution(mesh):
     in_specs = (
         P(("groups", "owner"), None),

time: 147 us -> 70.1 us (0.48); the launches traced: 145 us -> 69.8 us
  Pallas kernels: 18.8 us -> 63.4 us
  local copies, waits for them, and re-layouts: 47.4 us -> 5.14 us
  starting transfers between devices: 30.2 us -> 0 us
  waiting for transfers between devices: 29 us -> 0 us
  other arithmetic: 18.6 us -> 0.57 us
    pallas_call x0 -> x1, Pallas kernels: none -> 63.4 us  [fused_body(): pl.pallas_call(lambda *refs: owner_kernel(n, *refs), out_shape=(jax.Shape...]
    gather x7 -> x0, local copies, waits for them, and re-layouts: 30.9 us -> none  [the longest x1 6.87 us: body(): send_ids = jnp.where(slot_filled, target_local[source_pair], -1)]
    all_to_all x4 -> x0, starting transfers between devices: 30.2 us -> none  [the longest x1 11.2 us: body(): lax.all_to_all(live_sizes.astype(jnp.float32).reshape(source_count, slot_...]
    all_to_all x4 -> x0, waiting for transfers between devices: 29 us -> none  [the longest x1 18.5 us: body(): lax.all_to_all(masked_scores.reshape(source_count, slot_count, block_span...]
    another operation x1 -> x0, Pallas kernels: 17 us -> none
    sort x2 -> x0, other arithmetic: 8.73 us -> none  [the longest x1 4.37 us: body(): order = jnp.argsort(group_ids, stable=True)]
    unnamed x8 -> x9, local copies, waits for them, and re-layouts: 13.1 us -> 4.39 us
    select_n x9 -> x1, other arithmetic: 3.03 us -> 0.02 us  [slot_tables(): owner = flat_probes // clusters]
  transfers between devices with their start and end apart: 4 -> 0, of which waited for: 3 -> 0; matrix products, arithmetic and copies ran while one was open for 37% -> 0% of each run, Pallas kernels for 13% -> 0%
where the time goes in v1:
time: 70.1 us; the launch traced here: 69.8 us
  Pallas kernels  63.4 us (90%)
  local copies, waits for them, and re-layouts  5.14 us (7%)
    pallas_call x1, Pallas kernels, fused_body(): pl.pallas_call(lambda *refs: owner_kernel(n, *refs), out_shape=(jax.Shape...  63.4 us
    unnamed x9, local copies, waits for them, and re-layouts  4.39 us

profile of v1, /device:TPU:0, one launch (start us, length us, event | category | flops | bytes accessed | tf_op | source)
XLA Modules:
  0.0 69.8 jit_solution(940818483074342021)
XLA Ops:
  0.6 0.7 pad.4
  1.3 0.8 %copy.8 = s32[64,8]{1,0:T(8,128)S(1)} copy(s32[64,8]{0,1:T(8,128)} %param.6) | data formatting | bytes 4096 | tf_op args[1]
  2.1 0.1 reshape.118.refs_3_
  2.2 0.3 convert_reduce_fusion
  2.4 0.3 select_reduce_fusion
  2.7 0.0 copy-start
  2.8 0.9 %copy-done = bf16[64,1024]{1,0:T(8,128)(2,1)S(1)} copy-done((bf16[64,1024]{1,0:T(8,128)(2,1)S(1)}, bf16[64,1024]{1,0:T(8,128)(2,1)}, u32[]{:S(2)}) %copy-start) | copy-done | bytes 131096
  3.6 0.0 copy-start.1
  3.6 0.8 %copy-done.1 = bf16[16,1024]{1,0:T(8,128)(2,1)S(1)} copy-done((bf16[16,1024]{1,0:T(8,128)(2,1)S(1)}, bf16[16,1024]{1,0:T(8,128)(2,1)}, u32[]{:S(2)}) %copy-start.1) | copy-done | bytes 32792
  4.4 0.0 copy-start.2
  4.4 0.7 copy-done.2
  5.1 63.4 %shard_map.68 = (f32[64,8,256]{2,1,0:T(8,128)S(1)}, s32[64]{0:T(128)S(1)}) custom-call(bf16[64,1024]{1,0:T(8,128)(2,1)S(1)} %copy-done, s32[5,1,256]{2,1,0:T(1,128)S(1)} %pad_add_fusion.refs_1_, s32[512]{0:T(512)S(1)} %multiply_add_fusion.refs_2_, s32[512]{0:T(512)S(1)} %reshape.118.refs_3_, bf16[16,256,1024]{2,1,0:T(8,128)(2,1)} %refs_4_.1, ...), custom_call_target="tpu_custom_call" | custom-call | tf_op jit(solution)/shard_map/pallas_call | solution.py:386
  68.5 0.8 %copy.11 = f32[64,8,256]{2,1,0:T(8,128)} copy(f32[64,8,256]{2,1,0:T(8,128)S(1)} %get-tuple-element.6) | data formatting | bytes 1048576
  69.3 0.5 copy.12
  (3 shorter events, 0.0 us)
Async XLA Ops:
  2.7 0.9 %copy-start = (bf16[64,1024]{1,0:T(8,128)(2,1)S(1)}, bf16[64,1024]{1,0:T(8,128)(2,1)}, u32[]{:S(2)}) copy-start(bf16[64,1024]{1,0:T(8,128)(2,1)} %refs_0_.1) | copy-start | bytes 393220
  3.6 0.8 %copy-start.1 = (bf16[16,1024]{1,0:T(8,128)(2,1)S(1)}, bf16[16,1024]{1,0:T(8,128)(2,1)}, u32[]{:S(2)}) copy-start(bf16[16,1024]{1,0:T(8,128)(2,1)} %refs_5_.1) | copy-start | bytes 98308
  4.4 0.7 copy-start.2

commit v2 on v1

--- a/solution.py
+++ b/solution.py
@@ -82,13 +82,14 @@
 
 
 LANES = 128
+GROUP = 2
 TOP = 32767.0
 
 
 def owner_kernel(
-    n, q_ref, meta_ref, slot_ref, probe_ref, pass_ref, cent_ref, cnt_ref,
+    n, q_ref, meta_ref, code_ref, pass_ref, cent_ref, cnt_ref,
     out_ref, vis_ref,
-    pass_v, qs, ms, dense, picked, sendb, sends, recvb, recvs, code_s, cnt_s, scale_s,
+    pass_v, qs, ms, dense, picked, sendb, sends, recvb, recvs, words, factors, code_s, cnt_s, scale_s,
     pass_sem, qsend, msend, qrecv, mrecv, bsend, ssend, brecv, srecv, loc_sem,
 ):
     clusters, span, width = pass_ref.shape
@@ -97,7 +98,9 @@
     rows = 4 * per_device
     meta_rows, _, lane_count = meta_ref.shape
     cap = lane_count // 4
-    half = span // 2
+    parts = span // LANES
+    half = parts // 2
+    piece = per_device // 2
     me = lax.axis_index("owner")
     z = me // 4
     y = (me // 2) % 2
@@ -128,43 +131,48 @@
 
     pl.semaphore_wait(barrier, 2 + jnp.where(has_low, 1, 0) + jnp.where(has_high, 1, 0))
 
-    def pair(s, target, dev, own=False):
+    def pair(s, h, target, dev, own=False):
+        cut = pl.ds(h * piece, piece)
+        query_copy = pltpu.make_async_remote_copy(
+            src_ref=q_ref.at[cut] if own else qs.at[s, cut], dst_ref=qs.at[s, cut],
+            send_sem=qsend.at[s, h, target], recv_sem=qrecv.at[s, h], device_id={"owner": dev},
+        )
+        if h == 0:
+            return (query_copy,)
         return (
+            query_copy,
             pltpu.make_async_remote_copy(
                 src_ref=meta_ref if own else ms.at[s], dst_ref=ms.at[s],
                 send_sem=msend.at[s, target], recv_sem=mrecv.at[s], device_id={"owner": dev},
             ),
-            pltpu.make_async_remote_copy(
-                src_ref=q_ref if own else qs.at[s], dst_ref=qs.at[s],
-                send_sem=qsend.at[s, target], recv_sem=qrecv.at[s], device_id={"owner": dev},
-            ),
         )
 
-    def push(s, target, dev, own=False):
-        for copy in pair(s, target, dev, own):
+    def push(s, h, target, dev, own=False):
+        for copy in pair(s, h, target, dev, own):
             copy.start()
 
-    def drain(s, target, dev, own=False):
-        for copy in pair(s, target, dev, own):
+    def drain(s, h, target, dev, own=False):
+        for copy in pair(s, h, target, dev, own):
             copy.wait_send()
 
-    def arrive(s):
-        for copy in pair(s, 0, c_dev):
+    def arrive(s, h):
+        for copy in pair(s, h, 0, c_dev):
             copy.wait_recv()
 
-    def onward(act, s, low, high, own=False):
+    def onward(act, s, h, low, high, own=False):
         @pl.when(low)
         def _():
-            act(s, 0, me - 4, own)
+            act(s, h, 0, me - 4, own)
 
         @pl.when(high)
         def _():
-            act(s, 1, me + 4, own)
-
-        act(s, 2, y_dev, own)
-        act(s, 3, c_dev, own)
-
-    onward(push, me, has_low, has_high, True)
+            act(s, h, 1, me + 4, own)
+
+        act(s, h, 2, y_dev, own)
+        act(s, h, 3, c_dev, own)
+
+    for h in range(2):
+        onward(push, me, h, has_low, has_high, True)
     qs[me] = q_ref[...]
     ms[me] = meta_ref[...]
 
@@ -178,19 +186,21 @@
     def relay_z(k, act=push, wait=True):
         p = plane_of(k)
         s = p * 4 + y * 2 + c
-        if wait:
-            arrive(s)
-        onward(act, s, (p > z) & has_low, (p < z) & has_high)
+        for h in range(2):
+            if wait:
+                arrive(s, h)
+            onward(act, s, h, (p > z) & has_low, (p < z) & has_high)
 
     def relay_y(k):
         s = plane_of(k) * 4 + (1 - y) * 2 + c
-        arrive(s)
-        push(s, 3, c_dev)
+        for h in range(2):
+            arrive(s, h)
+            push(s, h, 3, c_dev)
 
     def back_pair(s):
         return (
             pltpu.make_async_remote_copy(
-                src_ref=sendb.at[s], dst_ref=recvb.at[me],
+                src_ref=sendb.at[pl.ds(s * cap, cap)], dst_ref=recvb.at[pl.ds(me * cap, cap)],
                 send_sem=bsend.at[s], recv_sem=brecv.at[me], device_id={"owner": s},
             ),
             pltpu.make_async_remote_copy(
@@ -218,22 +228,27 @@
         lane = lax.broadcasted_iota(jnp.int32, centre.shape, 1)
         slot_lane = lax.broadcasted_iota(jnp.int32, (1, span), 1)
 
-        def one_cluster(cl, carry):
-            @pl.when(k == 0)
-            def _():
-                pltpu.make_async_copy(pass_ref.at[cl], pass_v.at[cl], pass_sem.at[cl]).wait()
-
-            direct = lax.dot_general(
-                qs[pl.ds(base, 4)].reshape(rows, width), pass_v[cl],
-                (((1,), (1,)), ((), ())), preferred_element_type=jnp.float32,
-            )
-            term = jnp.sum(jnp.where(lane == cl, centre, 0.0), axis=1, keepdims=True)
-            dense[pl.ds(pl.multiple_of(cl * rows, rows), rows), :] = jnp.where(
-                slot_lane < cnt_ref[cl], direct + term, 0.0
-            )
+        def some_clusters(g, carry):
+            for u in range(GROUP):
+                cl = g * GROUP + u
+
+                @pl.when(k == 0)
+                def _():
+                    pltpu.make_async_copy(pass_ref.at[cl], pass_v.at[cl], pass_sem.at[cl]).wait()
+
+            for u in range(GROUP):
+                cl = g * GROUP + u
+                direct = lax.dot_general(
+                    qs[pl.ds(base, 4)].reshape(rows, width), pass_v[cl],
+                    (((1,), (1,)), ((), ())), preferred_element_type=jnp.float32,
+                )
+                term = jnp.sum(jnp.where(lane == cl, centre, 0.0), axis=1, keepdims=True)
+                scored = jnp.where(slot_lane < cnt_ref[cl], direct + term, 0.0)
+                for t in range(parts):
+                    dense[pl.ds(cl * rows, rows), t, :] = scored[:, t * LANES : (t + 1) * LANES]
             return carry
 
-        lax.fori_loop(0, clusters, one_cluster, 0)
+        lax.fori_loop(0, clusters // GROUP, some_clusters, 0)
         for i in range(4):
             for copy in to_scalar(base + i):
                 copy.wait()
@@ -244,15 +259,19 @@
                 for u in range(8):
                     k_slot = g * 8 + u
                     row = code_s[base + i, 0, code_lane + k_slot] + i * per_device
-                    picked[pl.ds(i * cap + k_slot, 1), :] = dense[pl.ds(row, 1), :]
+                    picked[i * cap + k_slot] = dense[row]
                 return carry
 
             lax.fori_loop(0, cap // 8, eight, 0)
-        found = picked[...]
-        top = jnp.maximum(jnp.max(jnp.abs(found), axis=1, keepdims=True), 1e-30)
-        coded = jnp.round(found * (TOP / top)).astype(jnp.int32)
-        packed = (coded[:, half:] << 16) | (coded[:, :half] & 0xFFFF)
-        sendb[pl.ds(base, 4)] = packed.reshape(4, cap, half)
+        found = [picked[:, t, :] for t in range(parts)]
+        peak = jnp.abs(found[0])
+        for t in range(1, parts):
+            peak = jnp.maximum(peak, jnp.abs(found[t]))
+        top = jnp.maximum(jnp.max(peak, axis=1, keepdims=True), 1e-30)
+        gain = TOP / top
+        coded = [jnp.round(part * gain).astype(jnp.int32) for part in found]
+        for t in range(half):
+            sendb[pl.ds(base * cap, 4 * cap), t, :] = (coded[half + t] << 16) | (coded[t] & 0xFFFF)
         wide = jnp.broadcast_to(top * (1.0 / TOP), (4 * cap, LANES))
         sends[p] = jnp.transpose(wide)[0:1, :]
         for i in range(4):
@@ -260,7 +279,7 @@
 
             @pl.when(s == me)
             def _():
-                recvb[me] = sendb[me]
+                recvb[pl.ds(me * cap, cap)] = sendb[pl.ds(me * cap, cap)]
                 recvs[me] = sends[p]
 
             @pl.when(s != me)
@@ -285,8 +304,9 @@
 
         relay_y(k)
         p = plane_of(k)
-        arrive(p * 4 + y * 2 + (1 - c))
-        arrive(p * 4 + (1 - y) * 2 + (1 - c))
+        for h in range(2):
+            arrive(p * 4 + y * 2 + (1 - c), h)
+            arrive(p * 4 + (1 - y) * 2 + (1 - c), h)
         compute(k)
         return carry
 
@@ -297,7 +317,7 @@
         def _():
             for copy in (
                 pltpu.make_async_remote_copy(
-                    src_ref=sendb.at[s], dst_ref=recvb.at[s],
+                    src_ref=sendb.at[pl.ds(s * cap, cap)], dst_ref=recvb.at[pl.ds(s * cap, cap)],
                     send_sem=bsend.at[s], recv_sem=brecv.at[s], device_id={"owner": c_dev},
                 ),
                 pltpu.make_async_remote_copy(
@@ -309,37 +329,51 @@
 
         return carry
 
+    def count_query(q, carry):
+        visited = jnp.int32(0)
+        for j in range(probe_count):
+            code = code_ref[q * probe_count + j]
+            visited = visited + cnt_s[code >> 16, 0, (code >> 8) & 255]
+        vis_ref[q] = visited
+        return carry
+
+    lax.fori_loop(0, per_device, count_query, 0)
     lax.fori_loop(0, n, collect, 0)
     scale_copy = pltpu.make_async_copy(recvs, scale_s, loc_sem.at[0, 0])
     scale_copy.start()
     scale_copy.wait()
-
-    def one_query(q, carry):
-        visited = jnp.int32(0)
+    scale_lane = (me % 4) * cap
+
+    def pick_query(q, carry):
         for j in range(probe_count):
-            slot = slot_ref[q * probe_count + j]
-            probe = probe_ref[q * probe_count + j]
-            owner = slot // cap
-            kept = slot % cap
-            scale = scale_s[owner, 0, (me % 4) * cap + kept]
-            word = recvb[owner, pl.ds(kept, 1), :]
-            low = (word << 16) >> 16
-            out_ref[q, j : j + 1, :half] = low.astype(jnp.float32) * scale
-            out_ref[q, j : j + 1, half:] = (word >> 16).astype(jnp.float32) * scale
-            visited = visited + cnt_s[probe // clusters, 0, probe % clusters]
-        vis_ref[q] = visited
-        return carry
-
-    lax.fori_loop(0, per_device, one_query, 0)
-
-    onward(drain, me, has_low, has_high, True)
+            code = code_ref[q * probe_count + j]
+            kept = code & 255
+            words[q * probe_count + j] = recvb[(code >> 16) * cap + kept]
+            factors[q * probe_count + j] = jnp.full(
+                (1, LANES), scale_s[code >> 16, 0, scale_lane + kept], jnp.float32
+            )
+        return carry
+
+    lax.fori_loop(0, per_device, pick_query, 0)
+    factor = factors[:, 0, :]
+    for t in range(half):
+        word = words[:, t, :]
+        low = ((word << 16) >> 16).astype(jnp.float32) * factor
+        high = (word >> 16).astype(jnp.float32) * factor
+        shape = (per_device, probe_count, LANES)
+        out_ref[:, :, t * LANES : (t + 1) * LANES] = low.reshape(shape)
+        out_ref[:, :, (half + t) * LANES : (half + t + 1) * LANES] = high.reshape(shape)
+
+    for h in range(2):
+        onward(drain, me, h, has_low, has_high, True)
 
     def finish(k, carry):
         @pl.when(k > 0)
         def _():
             relay_z(k, drain, False)
 
-        drain(plane_of(k) * 4 + (1 - y) * 2 + c, 3, c_dev)
+        for h in range(2):
+            drain(plane_of(k) * 4 + (1 - y) * 2 + c, h, 3, c_dev)
         return carry
 
     lax.fori_loop(0, planes, finish, 0)
@@ -365,7 +399,7 @@
     code = local * (4 * per_device) + pair // probe_count
     hit = slot[None, :] == jnp.arange(n * cap, dtype=jnp.int32)[:, None]
     table = jnp.sum(jnp.where(hit, code[None, :], 0), axis=1)
-    return slot, table
+    return (owner << 16) | (local << 8) | (slot - owner * cap), table
 
 
 def fused_body(queries, probes, passages, centroids, counts):
@@ -374,7 +408,7 @@
     clusters, span, width = passages.shape
     cap = 2 * per_device * probe_count // n
     flat = probes.reshape(-1)
-    slot, table = slot_tables(flat, n, cap, clusters, per_device, probe_count)
+    codes, table = slot_tables(flat, n, cap, clusters, per_device, probe_count)
     lane_count = 4 * cap
     count_row = jnp.pad(counts, (0, lane_count - clusters)).reshape(1, 1, lane_count)
     meta = jnp.concatenate([table.reshape(n // 4, 1, lane_count), count_row], axis=0)
@@ -382,32 +416,34 @@
     smem = pl.BlockSpec(memory_space=pltpu.SMEM)
     dma = pltpu.SemaphoreType.DMA
     rows = 4 * per_device
-    half = span // 2
+    parts = span // LANES
     return pl.pallas_call(
         lambda *refs: owner_kernel(n, *refs),
         out_shape=(
             jax.ShapeDtypeStruct((per_device, probe_count, span), jnp.float32),
             jax.ShapeDtypeStruct((per_device,), jnp.int32),
         ),
-        in_specs=[vmem, vmem, smem, smem, pl.BlockSpec(memory_space=pl.ANY), vmem, smem],
+        in_specs=[vmem, vmem, smem, pl.BlockSpec(memory_space=pl.ANY), vmem, smem],
         out_specs=(vmem, smem),
         scratch_shapes=[
             pltpu.VMEM((clusters, span, width), jnp.bfloat16),
             pltpu.VMEM((n, per_device, width), jnp.bfloat16),
             pltpu.VMEM((n, n // 4 + 1, 1, lane_count), jnp.int32),
-            pltpu.VMEM((clusters * rows, span), jnp.float32),
-            pltpu.VMEM((4 * cap, span), jnp.float32),
-            pltpu.VMEM((n, cap, half), jnp.int32),
+            pltpu.VMEM((clusters * rows, parts, LANES), jnp.float32),
+            pltpu.VMEM((4 * cap, parts, LANES), jnp.float32),
+            pltpu.VMEM((n * cap, parts // 2, LANES), jnp.int32),
             pltpu.VMEM((n // 4, 1, lane_count), jnp.float32),
-            pltpu.VMEM((n, cap, half), jnp.int32),
+            pltpu.VMEM((n * cap, parts // 2, LANES), jnp.int32),
             pltpu.VMEM((n, 1, lane_count), jnp.float32),
+            pltpu.VMEM((per_device * probe_count, parts // 2, LANES), jnp.int32),
+            pltpu.VMEM((per_device * probe_count, 1, LANES), jnp.float32),
             pltpu.SMEM((n, 1, lane_count), jnp.int32),
             pltpu.SMEM((n, 1, lane_count), jnp.int32),
             pltpu.SMEM((n, 1, lane_count), jnp.float32),
             dma((clusters,)),
+            dma((n, 2, 4)),
             dma((n, 4)),
-            dma((n, 4)),
-            dma((n,)),
+            dma((n, 2)),
             dma((n,)),
             dma((n,)),
             dma((n,)),
@@ -418,7 +454,7 @@
         compiler_params=pltpu.CompilerParams(
             collective_id=0, has_side_effects=True, vmem_limit_bytes=48 * 2**20
         ),
-    )(queries, meta, slot, flat, passages, centroids, counts)
+    )(queries, meta, codes, passages, centroids, counts)
 
 
 def body(queries, probes, passages, centroids, counts):
@@ -429,7 +465,8 @@
     held = clusters * span * (2 * width + 16 * per_device) + 2 * n * per_device * width
     fits = (
         n % 4 == 0 and n >= 8 and lane_count % LANES == 0 and lane_count >= clusters
-        and span % (2 * LANES) == 0 and held < 32 * 2**20
+        and span % (2 * LANES) == 0 and clusters % GROUP == 0 and clusters <= 256
+        and lane_count <= 1024 and per_device % 32 == 0 and held < 32 * 2**20
     )
     chosen = fused_body if fits else routed_body
     return chosen(queries, probes, passages, centroids, counts)

time: 70.1 us -> 66.6 us (0.950)
  Pallas kernels: 63.4 us -> 59.9 us
    pallas_call x1, Pallas kernels: 63.4 us -> 59.9 us  [fused_body(): pl.pallas_call(lambda *refs: owner_kernel(n, *refs), out_shape=(jax.Shape...]
where the time goes in v2:
time: 66.6 us; the launch traced here: 66.3 us
  Pallas kernels  59.9 us (90%)
  local copies, waits for them, and re-layouts  5.14 us (8%)
  between operations  0.67 us (1%)
    pallas_call x1, Pallas kernels, fused_body(): pl.pallas_call(lambda *refs: owner_kernel(n, *refs), out_shape=(jax.Shape...  59.9 us
    unnamed x9, local copies, waits for them, and re-layouts  4.39 us

profile of v2, /device:TPU:0, one launch (start us, length us, event | category | flops | bytes accessed | tf_op | source)
XLA Modules:
  0.0 66.3 jit_solution(7636642542997090483)
XLA Ops:
  0.6 0.7 pad.4
  1.3 0.8 %copy.8 = s32[64,8]{1,0:T(8,128)S(1)} copy(s32[64,8]{0,1:T(8,128)} %param.6) | data formatting | bytes 4096 | tf_op args[1]
  2.1 0.1 reshape.118
  2.2 0.3 convert_reduce_fusion
  2.4 0.3 select_reduce_fusion
  2.7 0.0 copy-start
  2.8 0.9 %copy-done = bf16[64,1024]{1,0:T(8,128)(2,1)S(1)} copy-done((bf16[64,1024]{1,0:T(8,128)(2,1)S(1)}, bf16[64,1024]{1,0:T(8,128)(2,1)}, u32[]{:S(2)}) %copy-start) | copy-done | bytes 131096
  3.7 0.0 copy-start.1
  3.7 0.8 %copy-done.1 = bf16[16,1024]{1,0:T(8,128)(2,1)S(1)} copy-done((bf16[16,1024]{1,0:T(8,128)(2,1)S(1)}, bf16[16,1024]{1,0:T(8,128)(2,1)}, u32[]{:S(2)}) %copy-start.1) | copy-done | bytes 32792
  4.4 0.0 copy-start.2
  4.4 0.7 copy-done.2
  5.1 59.9 %shard_map.68 = (f32[64,8,256]{2,1,0:T(8,128)S(1)}, s32[64]{0:T(128)S(1)}) custom-call(bf16[64,1024]{1,0:T(8,128)(2,1)S(1)} %copy-done, s32[5,1,256]{2,1,0:T(1,128)S(1)} %pad_add_fusion.refs_1_, s32[512]{0:T(512)S(1)} %get-tuple-element.2.refs_2_, bf16[16,256,1024]{2,1,0:T(8,128)(2,1)} %refs_3_.1, bf16[16,1024]{1,0:T(8,128)(2,1)S(1)} %copy-done.1, ...), custom_call_target="tpu_custom_call" | custom-call | tf_op jit(solution)/shard_map/pallas_call | solution.py:420
  65.0 0.8 %copy.11 = f32[64,8,256]{2,1,0:T(8,128)} copy(f32[64,8,256]{2,1,0:T(8,128)S(1)} %get-tuple-element.7) | data formatting | bytes 1048576
  65.8 0.5 copy.12
  (3 shorter events, 0.0 us)
Async XLA Ops:
  2.7 0.9 %copy-start = (bf16[64,1024]{1,0:T(8,128)(2,1)S(1)}, bf16[64,1024]{1,0:T(8,128)(2,1)}, u32[]{:S(2)}) copy-start(bf16[64,1024]{1,0:T(8,128)(2,1)} %refs_0_.1) | copy-start | bytes 393220
  3.7 0.8 %copy-start.1 = (bf16[16,1024]{1,0:T(8,128)(2,1)S(1)}, bf16[16,1024]{1,0:T(8,128)(2,1)}, u32[]{:S(2)}) copy-start(bf16[16,1024]{1,0:T(8,128)(2,1)} %refs_4_.1) | copy-start | bytes 98308
  4.4 0.7 copy-start.2

commit v3 on v2

--- a/solution.py
+++ b/solution.py
@@ -107,8 +107,6 @@
     c = me % 2
     y_dev = z * 4 + (1 - y) * 2 + c
     c_dev = z * 4 + y * 2 + (1 - c)
-    has_low = z > 0
-    has_high = z < planes - 1
 
     for k in range(clusters):
         pltpu.make_async_copy(pass_ref.at[k], pass_v.at[k], pass_sem.at[k]).start()
@@ -121,15 +119,12 @@
     greet(y_dev)
     greet(c_dev)
 
-    @pl.when(has_low)
-    def _():
-        greet(me - 4)
-
-    @pl.when(has_high)
-    def _():
-        greet(me + 4)
-
-    pl.semaphore_wait(barrier, 2 + jnp.where(has_low, 1, 0) + jnp.where(has_high, 1, 0))
+    for p in range(planes):
+        @pl.when(p != z)
+        def _():
+            greet(p * 4 + y * 2 + c)
+
+    pl.semaphore_wait(barrier, planes + 1)
 
     def pair(s, h, target, dev, own=False):
         cut = pl.ds(h * piece, piece)
@@ -159,20 +154,21 @@
         for copy in pair(s, h, 0, c_dev):
             copy.wait_recv()
 
-    def onward(act, s, h, low, high, own=False):
-        @pl.when(low)
-        def _():
-            act(s, h, 0, me - 4, own)
-
-        @pl.when(high)
-        def _():
-            act(s, h, 1, me + 4, own)
-
-        act(s, h, 2, y_dev, own)
-        act(s, h, 3, c_dev, own)
-
-    for h in range(2):
-        onward(push, me, h, has_low, has_high, True)
+    def onward(act, s, h, own=False):
+        act(s, h, planes, y_dev, own)
+        act(s, h, planes + 1, c_dev, own)
+
+    def spread(act):
+        for h in range(2):
+            onward(act, me, h, True)
+        for d in range(1, planes):
+            for p in (z - d, z + d):
+                @pl.when((p >= 0) & (p < planes))
+                def _():
+                    for h in range(2):
+                        act(me, h, p, p * 4 + y * 2 + c, True)
+
+    spread(push)
     qs[me] = q_ref[...]
     ms[me] = meta_ref[...]
 
@@ -189,13 +185,13 @@
         for h in range(2):
             if wait:
                 arrive(s, h)
-            onward(act, s, h, (p > z) & has_low, (p < z) & has_high)
+            onward(act, s, h)
 
     def relay_y(k):
         s = plane_of(k) * 4 + (1 - y) * 2 + c
         for h in range(2):
             arrive(s, h)
-            push(s, h, 3, c_dev)
+            push(s, h, planes + 1, c_dev)
 
     def back_pair(s):
         return (
@@ -209,18 +205,15 @@
             ),
         )
 
-    def to_scalar(s):
-        return (
-            pltpu.make_async_copy(ms.at[s, me // 4], code_s.at[s], loc_sem.at[0, s]),
-            pltpu.make_async_copy(ms.at[s, meta_rows - 1], cnt_s.at[s], loc_sem.at[1, s]),
+    def to_scalar(p):
+        return pltpu.make_async_copy(
+            ms.at[pl.ds(p * 4, 4), me // 4], code_s.at[pl.ds(p * 4, 4)], loc_sem.at[p]
         )
 
     def compute(k):
         p = plane_of(k)
         base = p * 4
-        for i in range(4):
-            for copy in to_scalar(base + i):
-                copy.start()
+        to_scalar(p).start()
         block = qs[pl.ds(base, 4)].reshape(rows, width)
         centre = lax.dot_general(
             block, cent_ref[...], (((1,), (1,)), ((), ())), preferred_element_type=jnp.float32
@@ -249,9 +242,7 @@
             return carry
 
         lax.fori_loop(0, clusters // GROUP, some_clusters, 0)
-        for i in range(4):
-            for copy in to_scalar(base + i):
-                copy.wait()
+        to_scalar(p).wait()
         for i in range(4):
             code_lane = (me % 4) * cap
 
@@ -287,20 +278,10 @@
                 for copy in back_pair(s):
                     copy.start()
 
-    ahead = 1 + jnp.where(near >= 1, 1, 0)
-
     def step(k, carry):
-        @pl.when((k == 0) & (planes > 1))
+        @pl.when(k + 1 < planes)
         def _():
-            relay_z(1)
-
-        @pl.when((k == 0) & (ahead > 1))
-        def _():
-            relay_z(2)
-
-        @pl.when((k > 0) & (k + ahead < planes))
-        def _():
-            relay_z(k + ahead)
+            relay_z(k + 1)
 
         relay_y(k)
         p = plane_of(k)
@@ -337,9 +318,12 @@
         vis_ref[q] = visited
         return carry
 
+    count_copy = pltpu.make_async_copy(ms.at[:, meta_rows - 1], cnt_s, loc_sem.at[0])
+    count_copy.start()
+    count_copy.wait()
     lax.fori_loop(0, per_device, count_query, 0)
     lax.fori_loop(0, n, collect, 0)
-    scale_copy = pltpu.make_async_copy(recvs, scale_s, loc_sem.at[0, 0])
+    scale_copy = pltpu.make_async_copy(recvs, scale_s, loc_sem.at[0])
     scale_copy.start()
     scale_copy.wait()
     scale_lane = (me % 4) * cap
@@ -364,8 +348,7 @@
         out_ref[:, :, t * LANES : (t + 1) * LANES] = low.reshape(shape)
         out_ref[:, :, (half + t) * LANES : (half + t + 1) * LANES] = high.reshape(shape)
 
-    for h in range(2):
-        onward(drain, me, h, has_low, has_high, True)
+    spread(drain)
 
     def finish(k, carry):
         @pl.when(k > 0)
@@ -373,7 +356,7 @@
             relay_z(k, drain, False)
 
         for h in range(2):
-            drain(plane_of(k) * 4 + (1 - y) * 2 + c, h, 3, c_dev)
+            drain(plane_of(k) * 4 + (1 - y) * 2 + c, h, planes + 1, c_dev)
         return carry
 
     lax.fori_loop(0, planes, finish, 0)
@@ -441,15 +424,15 @@
             pltpu.SMEM((n, 1, lane_count), jnp.int32),
             pltpu.SMEM((n, 1, lane_count), jnp.float32),
             dma((clusters,)),
-            dma((n, 2, 4)),
-            dma((n, 4)),
+            dma((n, 2, n // 4 + 2)),
+            dma((n, n // 4 + 2)),
             dma((n, 2)),
             dma((n,)),
             dma((n,)),
             dma((n,)),
             dma((n,)),
             dma((n,)),
-            dma((2, n)),
+            dma((n // 4,)),
         ],
         compiler_params=pltpu.CompilerParams(
             collective_id=0, has_side_effects=True, vmem_limit_bytes=48 * 2**20

time: 66.6 us -> 70.9 us (1.065)
  Pallas kernels: 59.9 us -> 64.3 us
    pallas_call x1, Pallas kernels: 59.9 us -> 64.3 us  [fused_body(): pl.pallas_call(lambda *refs: owner_kernel(n, *refs), out_shape=(jax.Shape...]
where the time goes in v3:
time: 70.9 us; the launch traced here: 70.7 us
  Pallas kernels  64.3 us (91%)
  local copies, waits for them, and re-layouts  5.14 us (7%)
    pallas_call x1, Pallas kernels, fused_body(): pl.pallas_call(lambda *refs: owner_kernel(n, *refs), out_shape=(jax.Shape...  64.3 us
    unnamed x9, local copies, waits for them, and re-layouts  4.39 us

profile of v3, /device:TPU:0, one launch (start us, length us, event | category | flops | bytes accessed | tf_op | source)
XLA Modules:
  0.0 70.7 jit_solution(3642462687266207426)
XLA Ops:
  0.6 0.7 pad.4
  1.3 0.8 %copy.8 = s32[64,8]{1,0:T(8,128)S(1)} copy(s32[64,8]{0,1:T(8,128)} %param.6) | data formatting | bytes 4096 | tf_op args[1]
  2.1 0.1 reshape.118
  2.2 0.3 convert_reduce_fusion
  2.4 0.3 select_reduce_fusion
  2.7 0.0 copy-start
  2.8 0.9 %copy-done = bf16[64,1024]{1,0:T(8,128)(2,1)S(1)} copy-done((bf16[64,1024]{1,0:T(8,128)(2,1)S(1)}, bf16[64,1024]{1,0:T(8,128)(2,1)}, u32[]{:S(2)}) %copy-start) | copy-done | bytes 131096
  3.7 0.0 copy-start.1
  3.7 0.8 %copy-done.1 = bf16[16,1024]{1,0:T(8,128)(2,1)S(1)} copy-done((bf16[16,1024]{1,0:T(8,128)(2,1)S(1)}, bf16[16,1024]{1,0:T(8,128)(2,1)}, u32[]{:S(2)}) %copy-start.1) | copy-done | bytes 32792
  4.4 0.0 copy-start.2
  4.4 0.7 copy-done.2
  5.1 64.3 %shard_map.68 = (f32[64,8,256]{2,1,0:T(8,128)S(1)}, s32[64]{0:T(128)S(1)}) custom-call(bf16[64,1024]{1,0:T(8,128)(2,1)S(1)} %copy-done, s32[5,1,256]{2,1,0:T(1,128)S(1)} %pad_add_fusion.refs_1_, s32[512]{0:T(512)S(1)} %get-tuple-element.2.refs_2_, bf16[16,256,1024]{2,1,0:T(8,128)(2,1)} %refs_3_.1, bf16[16,1024]{1,0:T(8,128)(2,1)S(1)} %copy-done.1, ...), custom_call_target="tpu_custom_call" | custom-call | tf_op jit(solution)/shard_map/pallas_call | solution.py:403
  69.4 0.8 %copy.11 = f32[64,8,256]{2,1,0:T(8,128)} copy(f32[64,8,256]{2,1,0:T(8,128)S(1)} %get-tuple-element.7) | data formatting | bytes 1048576
  70.2 0.5 copy.12
  (3 shorter events, 0.0 us)
Async XLA Ops:
  2.7 0.9 %copy-start = (bf16[64,1024]{1,0:T(8,128)(2,1)S(1)}, bf16[64,1024]{1,0:T(8,128)(2,1)}, u32[]{:S(2)}) copy-start(bf16[64,1024]{1,0:T(8,128)(2,1)} %refs_0_.1) | copy-start | bytes 393220
  3.7 0.8 %copy-start.1 = (bf16[16,1024]{1,0:T(8,128)(2,1)S(1)}, bf16[16,1024]{1,0:T(8,128)(2,1)}, u32[]{:S(2)}) copy-start(bf16[16,1024]{1,0:T(8,128)(2,1)} %refs_4_.1) | copy-start | bytes 98308
  4.4 0.7 copy-start.2

commit v4 on v2

--- a/solution.py
+++ b/solution.py
@@ -82,7 +82,6 @@
 
 
 LANES = 128
-GROUP = 2
 TOP = 32767.0
 
 
@@ -95,7 +94,7 @@
     clusters, span, width = pass_ref.shape
     per_device, probe_count, _ = out_ref.shape
     planes = n // 4
-    rows = 4 * per_device
+    rows = n * per_device
     meta_rows, _, lane_count = meta_ref.shape
     cap = lane_count // 4
     parts = span // LANES
@@ -209,56 +208,44 @@
             ),
         )
 
-    def to_scalar(s):
-        return (
-            pltpu.make_async_copy(ms.at[s, me // 4], code_s.at[s], loc_sem.at[0, s]),
-            pltpu.make_async_copy(ms.at[s, meta_rows - 1], cnt_s.at[s], loc_sem.at[1, s]),
+    def to_scalar(p):
+        return pltpu.make_async_copy(
+            ms.at[pl.ds(p * 4, 4), me // 4], code_s.at[pl.ds(p * 4, 4)], loc_sem.at[p]
         )
 
-    def compute(k):
-        p = plane_of(k)
-        base = p * 4
-        for i in range(4):
-            for copy in to_scalar(base + i):
-                copy.start()
-        block = qs[pl.ds(base, 4)].reshape(rows, width)
+    def multiply():
+        block = qs[...].reshape(rows, width)
         centre = lax.dot_general(
             block, cent_ref[...], (((1,), (1,)), ((), ())), preferred_element_type=jnp.float32
         )
         lane = lax.broadcasted_iota(jnp.int32, centre.shape, 1)
         slot_lane = lax.broadcasted_iota(jnp.int32, (1, span), 1)
 
-        def some_clusters(g, carry):
-            for u in range(GROUP):
-                cl = g * GROUP + u
-
-                @pl.when(k == 0)
-                def _():
-                    pltpu.make_async_copy(pass_ref.at[cl], pass_v.at[cl], pass_sem.at[cl]).wait()
-
-            for u in range(GROUP):
-                cl = g * GROUP + u
-                direct = lax.dot_general(
-                    qs[pl.ds(base, 4)].reshape(rows, width), pass_v[cl],
-                    (((1,), (1,)), ((), ())), preferred_element_type=jnp.float32,
-                )
-                term = jnp.sum(jnp.where(lane == cl, centre, 0.0), axis=1, keepdims=True)
-                scored = jnp.where(slot_lane < cnt_ref[cl], direct + term, 0.0)
-                for t in range(parts):
-                    dense[pl.ds(cl * rows, rows), t, :] = scored[:, t * LANES : (t + 1) * LANES]
+        def one_cluster(cl, carry):
+            pltpu.make_async_copy(pass_ref.at[cl], pass_v.at[cl], pass_sem.at[cl]).wait()
+            direct = lax.dot_general(
+                qs[...].reshape(rows, width), pass_v[cl],
+                (((1,), (1,)), ((), ())), preferred_element_type=jnp.float32,
+            )
+            term = jnp.sum(jnp.where(lane == cl, centre, 0.0), axis=1, keepdims=True)
+            scored = jnp.where(slot_lane < cnt_ref[cl], direct + term, 0.0)
+            for t in range(parts):
+                dense[pl.ds(cl * rows, rows), t, :] = scored[:, t * LANES : (t + 1) * LANES]
             return carry
 
-        lax.fori_loop(0, clusters // GROUP, some_clusters, 0)
-        for i in range(4):
-            for copy in to_scalar(base + i):
-                copy.wait()
+        lax.fori_loop(0, clusters, one_cluster, 0)
+
+    def compute(k):
+        p = plane_of(planes - 1 - k)
+        base = p * 4
+        to_scalar(p).wait()
         for i in range(4):
             code_lane = (me % 4) * cap
 
             def eight(g, carry):
                 for u in range(8):
                     k_slot = g * 8 + u
-                    row = code_s[base + i, 0, code_lane + k_slot] + i * per_device
+                    row = code_s[base + i, 0, code_lane + k_slot] + (base + i) * per_device
                     picked[i * cap + k_slot] = dense[row]
                 return carry
 
@@ -307,10 +294,17 @@
         for h in range(2):
             arrive(p * 4 + y * 2 + (1 - c), h)
             arrive(p * 4 + (1 - y) * 2 + (1 - c), h)
+        to_scalar(p).start()
+        return carry
+
+    lax.fori_loop(0, planes, step, 0)
+    multiply()
+
+    def answer(k, carry):
         compute(k)
         return carry
 
-    lax.fori_loop(0, planes, step, 0)
+    lax.fori_loop(0, planes, answer, 0)
 
     def collect(s, carry):
         @pl.when(s != me)
@@ -337,9 +331,12 @@
         vis_ref[q] = visited
         return carry
 
+    count_copy = pltpu.make_async_copy(ms.at[:, meta_rows - 1], cnt_s, loc_sem.at[0])
+    count_copy.start()
+    count_copy.wait()
     lax.fori_loop(0, per_device, count_query, 0)
     lax.fori_loop(0, n, collect, 0)
-    scale_copy = pltpu.make_async_copy(recvs, scale_s, loc_sem.at[0, 0])
+    scale_copy = pltpu.make_async_copy(recvs, scale_s, loc_sem.at[0])
     scale_copy.start()
     scale_copy.wait()
     scale_lane = (me % 4) * cap
@@ -396,7 +393,7 @@
     pair = jnp.arange(pair_count, dtype=jnp.int32)
     same = (owner[:, None] == owner[None, :]) & (pair[None, :] < pair[:, None])
     slot = owner * cap + jnp.sum(same.astype(jnp.int32), axis=1)
-    code = local * (4 * per_device) + pair // probe_count
+    code = local * (n * per_device) + pair // probe_count
     hit = slot[None, :] == jnp.arange(n * cap, dtype=jnp.int32)[:, None]
     table = jnp.sum(jnp.where(hit, code[None, :], 0), axis=1)
     return (owner << 16) | (local << 8) | (slot - owner * cap), table
@@ -415,7 +412,7 @@
     vmem = pl.BlockSpec(memory_space=pltpu.VMEM)
     smem = pl.BlockSpec(memory_space=pltpu.SMEM)
     dma = pltpu.SemaphoreType.DMA
-    rows = 4 * per_device
+    rows = n * per_device
     parts = span // LANES
     return pl.pallas_call(
         lambda *refs: owner_kernel(n, *refs),
@@ -449,7 +446,7 @@
             dma((n,)),
             dma((n,)),
             dma((n,)),
-            dma((2, n)),
+            dma((n // 4,)),
         ],
         compiler_params=pltpu.CompilerParams(
             collective_id=0, has_side_effects=True, vmem_limit_bytes=48 * 2**20
@@ -462,10 +459,10 @@
     per_device, probe_count = probes.shape
     clusters, span, width = passages.shape
     lane_count = 8 * per_device * probe_count // n
-    held = clusters * span * (2 * width + 16 * per_device) + 2 * n * per_device * width
+    held = clusters * span * (2 * width + 4 * n * per_device) + 2 * n * per_device * width
     fits = (
         n % 4 == 0 and n >= 8 and lane_count % LANES == 0 and lane_count >= clusters
-        and span % (2 * LANES) == 0 and clusters % GROUP == 0 and clusters <= 256
+        and span % (2 * LANES) == 0 and clusters <= 256
         and lane_count <= 1024 and per_device % 32 == 0 and held < 32 * 2**20
     )
     chosen = fused_body if fits else routed_body

time: 66.6 us -> 67.1 us (level)
  the two profiles are of different devices: /device:TPU:0 before, /device:TPU:13 now
where the time goes in v4:
time: 67.1 us; the launch traced here: 66.8 us
  Pallas kernels  60.4 us (90%)
  local copies, waits for them, and re-layouts  5.14 us (8%)
    pallas_call x1, Pallas kernels, fused_body(): pl.pallas_call(lambda *refs: owner_kernel(n, *refs), out_shape=(jax.Shape...  60.4 us
    unnamed x9, local copies, waits for them, and re-layouts  4.39 us

profile of v4, /device:TPU:13, one launch (start us, length us, event | category | flops | bytes accessed | tf_op | source)
XLA Modules:
  0.0 66.8 jit_solution(3624168378807547392)
XLA Ops:
  0.6 0.7 pad.4
  1.3 0.8 %copy.8 = s32[64,8]{1,0:T(8,128)S(1)} copy(s32[64,8]{0,1:T(8,128)} %param.6) | data formatting | bytes 4096 | tf_op args[1]
  2.1 0.1 reshape.118
  2.2 0.3 convert_reduce_fusion
  2.4 0.3 select_reduce_fusion
  2.7 0.0 copy-start
  2.8 0.9 %copy-done = bf16[64,1024]{1,0:T(8,128)(2,1)S(1)} copy-done((bf16[64,1024]{1,0:T(8,128)(2,1)S(1)}, bf16[64,1024]{1,0:T(8,128)(2,1)}, u32[]{:S(2)}) %copy-start) | copy-done | bytes 131096
  3.7 0.0 copy-start.1
  3.7 0.8 %copy-done.1 = bf16[16,1024]{1,0:T(8,128)(2,1)S(1)} copy-done((bf16[16,1024]{1,0:T(8,128)(2,1)S(1)}, bf16[16,1024]{1,0:T(8,128)(2,1)}, u32[]{:S(2)}) %copy-start.1) | copy-done | bytes 32792
  4.4 0.0 copy-start.2
  4.4 0.7 copy-done.2
  5.1 60.4 %shard_map.68 = (f32[64,8,256]{2,1,0:T(8,128)S(1)}, s32[64]{0:T(128)S(1)}) custom-call(bf16[64,1024]{1,0:T(8,128)(2,1)S(1)} %copy-done, s32[5,1,256]{2,1,0:T(1,128)S(1)} %pad_add_fusion.refs_1_, s32[512]{0:T(512)S(1)} %get-tuple-element.2.refs_2_, bf16[16,256,1024]{2,1,0:T(8,128)(2,1)} %refs_3_.1, bf16[16,1024]{1,0:T(8,128)(2,1)S(1)} %copy-done.1, ...), custom_call_target="tpu_custom_call" | custom-call | tf_op jit(solution)/shard_map/pallas_call | solution.py:417
  65.5 0.8 %copy.11 = f32[64,8,256]{2,1,0:T(8,128)} copy(f32[64,8,256]{2,1,0:T(8,128)S(1)} %get-tuple-element.7) | data formatting | bytes 1048576
  66.3 0.5 copy.12
  (3 shorter events, 0.0 us)
Async XLA Ops:
  2.7 0.9 %copy-start = (bf16[64,1024]{1,0:T(8,128)(2,1)S(1)}, bf16[64,1024]{1,0:T(8,128)(2,1)}, u32[]{:S(2)}) copy-start(bf16[64,1024]{1,0:T(8,128)(2,1)} %refs_0_.1) | copy-start | bytes 393220
  3.7 0.8 %copy-start.1 = (bf16[16,1024]{1,0:T(8,128)(2,1)S(1)}, bf16[16,1024]{1,0:T(8,128)(2,1)}, u32[]{:S(2)}) copy-start(bf16[16,1024]{1,0:T(8,128)(2,1)} %refs_4_.1) | copy-start | bytes 98308
  4.4 0.7 copy-start.2

commit v5 on v4

--- a/solution.py
+++ b/solution.py
@@ -208,9 +208,13 @@
             ),
         )
 
+    my_lane = (me % 4) * cap
+    my_lanes = pl.ds(pl.multiple_of(my_lane // LANES * LANES, LANES), LANES)
+    my_rest = my_lane % LANES
+
     def to_scalar(p):
         return pltpu.make_async_copy(
-            ms.at[pl.ds(p * 4, 4), me // 4], code_s.at[pl.ds(p * 4, 4)], loc_sem.at[p]
+            ms.at[pl.ds(p * 4, 4), me // 4, :, my_lanes], code_s.at[pl.ds(p * 4, 4)], loc_sem.at[p]
         )
 
     def multiply():
@@ -240,7 +244,7 @@
         base = p * 4
         to_scalar(p).wait()
         for i in range(4):
-            code_lane = (me % 4) * cap
+            code_lane = my_rest
 
             def eight(g, carry):
                 for u in range(8):
@@ -331,15 +335,15 @@
         vis_ref[q] = visited
         return carry
 
-    count_copy = pltpu.make_async_copy(ms.at[:, meta_rows - 1], cnt_s, loc_sem.at[0])
+    count_copy = pltpu.make_async_copy(ms.at[:, meta_rows - 1, :, pl.ds(0, LANES)], cnt_s, loc_sem.at[0])
     count_copy.start()
     count_copy.wait()
     lax.fori_loop(0, per_device, count_query, 0)
     lax.fori_loop(0, n, collect, 0)
-    scale_copy = pltpu.make_async_copy(recvs, scale_s, loc_sem.at[0])
+    scale_copy = pltpu.make_async_copy(recvs.at[:, :, my_lanes], scale_s, loc_sem.at[0])
     scale_copy.start()
     scale_copy.wait()
-    scale_lane = (me % 4) * cap
+    scale_lane = my_rest
 
     def pick_query(q, carry):
         for j in range(probe_count):
@@ -434,9 +438,9 @@
             pltpu.VMEM((n, 1, lane_count), jnp.float32),
             pltpu.VMEM((per_device * probe_count, parts // 2, LANES), jnp.int32),
             pltpu.VMEM((per_device * probe_count, 1, LANES), jnp.float32),
-            pltpu.SMEM((n, 1, lane_count), jnp.int32),
-            pltpu.SMEM((n, 1, lane_count), jnp.int32),
-            pltpu.SMEM((n, 1, lane_count), jnp.float32),
+            pltpu.SMEM((n, 1, LANES), jnp.int32),
+            pltpu.SMEM((n, 1, LANES), jnp.int32),
+            pltpu.SMEM((n, 1, LANES), jnp.float32),
             dma((clusters,)),
             dma((n, 2, 4)),
             dma((n, 4)),
@@ -462,7 +466,7 @@
     held = clusters * span * (2 * width + 4 * n * per_device) + 2 * n * per_device * width
     fits = (
         n % 4 == 0 and n >= 8 and lane_count % LANES == 0 and lane_count >= clusters
-        and span % (2 * LANES) == 0 and clusters <= 256
+        and span % (2 * LANES) == 0 and clusters <= LANES and LANES % (lane_count // 4) == 0
         and lane_count <= 1024 and per_device % 32 == 0 and held < 32 * 2**20
     )
     chosen = fused_body if fits else routed_body

time: 67.1 us -> 66.8 us (level)
  no operation moved by 1% of the time
where the time goes in v5:
time: 66.8 us; the launch traced here: 66.6 us
  Pallas kernels  60.2 us (90%)
  local copies, waits for them, and re-layouts  5.14 us (8%)
  between operations  0.67 us (1%)
    pallas_call x1, Pallas kernels, fused_body(): pl.pallas_call(lambda *refs: owner_kernel(n, *refs), out_shape=(jax.Shape...  60.2 us
    unnamed x9, local copies, waits for them, and re-layouts  4.39 us

profile of v5, /device:TPU:13, one launch (start us, length us, event | category | flops | bytes accessed | tf_op | source)
XLA Modules:
  0.0 66.6 jit_solution(16956119417207239833)
XLA Ops:
  0.6 0.7 pad.4
  1.3 0.8 %copy.8 = s32[64,8]{1,0:T(8,128)S(1)} copy(s32[64,8]{0,1:T(8,128)} %param.6) | data formatting | bytes 4096 | tf_op args[1]
  2.1 0.1 reshape.118
  2.2 0.3 convert_reduce_fusion
  2.4 0.3 select_reduce_fusion
  2.7 0.0 copy-start
  2.8 0.9 %copy-done = bf16[64,1024]{1,0:T(8,128)(2,1)S(1)} copy-done((bf16[64,1024]{1,0:T(8,128)(2,1)S(1)}, bf16[64,1024]{1,0:T(8,128)(2,1)}, u32[]{:S(2)}) %copy-start) | copy-done | bytes 131096
  3.7 0.0 copy-start.1
  3.7 0.8 %copy-done.1 = bf16[16,1024]{1,0:T(8,128)(2,1)S(1)} copy-done((bf16[16,1024]{1,0:T(8,128)(2,1)S(1)}, bf16[16,1024]{1,0:T(8,128)(2,1)}, u32[]{:S(2)}) %copy-start.1) | copy-done | bytes 32792
  4.4 0.0 copy-start.2
  4.4 0.7 copy-done.2
  5.1 60.2 %shard_map.68 = (f32[64,8,256]{2,1,0:T(8,128)S(1)}, s32[64]{0:T(128)S(1)}) custom-call(bf16[64,1024]{1,0:T(8,128)(2,1)S(1)} %copy-done, s32[5,1,256]{2,1,0:T(1,128)S(1)} %pad_add_fusion.refs_1_, s32[512]{0:T(512)S(1)} %get-tuple-element.2.refs_2_, bf16[16,256,1024]{2,1,0:T(8,128)(2,1)} %refs_3_.1, bf16[16,1024]{1,0:T(8,128)(2,1)S(1)} %copy-done.1, ...), custom_call_target="tpu_custom_call" | custom-call | tf_op jit(solution)/shard_map/pallas_call | solution.py:421
  65.3 0.8 %copy.11 = f32[64,8,256]{2,1,0:T(8,128)} copy(f32[64,8,256]{2,1,0:T(8,128)S(1)} %get-tuple-element.7) | data formatting | bytes 1048576
  66.1 0.5 copy.12
  (3 shorter events, 0.0 us)
Async XLA Ops:
  2.7 0.9 %copy-start = (bf16[64,1024]{1,0:T(8,128)(2,1)S(1)}, bf16[64,1024]{1,0:T(8,128)(2,1)}, u32[]{:S(2)}) copy-start(bf16[64,1024]{1,0:T(8,128)(2,1)} %refs_0_.1) | copy-start | bytes 393220
  3.7 0.8 %copy-start.1 = (bf16[16,1024]{1,0:T(8,128)(2,1)S(1)}, bf16[16,1024]{1,0:T(8,128)(2,1)}, u32[]{:S(2)}) copy-start(bf16[16,1024]{1,0:T(8,128)(2,1)} %refs_4_.1) | copy-start | bytes 98308
  4.4 0.7 copy-start.2
